TPU v7x, 32 devices: a whole 2x2x4 slice. The times are simulated.
32 devices in a mesh: dp: 8 (over z, x), expert: 4 (over y, core).
Axes of the slice: x: 2, y: 2, z: 4, core: 2. Of those that a mesh axis runs over, the one named last changes fastest.
Arguments:
- tokens: bfloat16 [4096, 4096], P(('dp', 'expert')), may hold values from -6 to 6
- grad_out: bfloat16 [4096, 4096], P(('dp', 'expert')), may hold values from -6 to 6
- experts: int32 [4096, 2], P(('dp', 'expert')), may hold values from 0 to 7, all different within a row; in each aligned block of 128 rows (0 to 127, 128 to 255, ...) at most 64 rows name the same one
- gates: bfloat16 [4096, 2], P(('dp', 'expert')), may hold values from 0 to 1, as said below
- router_weight: bfloat16 [8, 4096], replicated, may hold values from -3 to 3
- saved_outputs: bfloat16 [16384, 4096], P(('dp', 'expert')), may hold values from -0.19921875 to 0.19921875
Outputs:
- input_grad: bfloat16 [4096, 4096], P(('dp', 'expert'))
- router_grad: float32 [8, 4096], replicated
- expert_grad: bfloat16 [16384, 4096], P(('dp', 'expert'))
Inputs may be any that keep to these rules, and one draw needn't show every extreme that they name: Within each aligned block of 128 tokens (the tokens of one device), no expert is named by more than 64 slots, and in some blocks an expert is named by exactly 64 slots. The two experts of a token differ. The two gates of a token are positive and add up to one, up to rounding to bfloat16.
All inputs are finite; a program needn't handle non-finite values.
Results may differ from a plain program's by a relative error of at most 0.0085.
Values may be sent and summed in bfloat16 or wider, within the bound.
A program may use at most 64 MiB of HBM per device.

v0:
```python
import jax
import jax.numpy as jnp
from jax import lax
from jax.sharding import PartitionSpec as P


def slot_positions(experts, count):
    slot_expert = experts.reshape(-1)
    onehot = (slot_expert[:, None] == jnp.arange(count, dtype=jnp.int32)[None, :]).astype(jnp.int32)
    before = jnp.cumsum(onehot, axis=0) - onehot
    return (slot_expert, jnp.sum(before * onehot, axis=1))


def local(tokens, grad_out, experts, gates, router_weight, saved_outputs):
    groups = lax.axis_size("expert")
    chosen_count = experts.shape[1]
    expert_count = router_weight.shape[0]
    held = expert_count // groups
    capacity = tokens.shape[0] // 2
    width = saved_outputs.shape[1]
    slot_expert, position = slot_positions(experts, expert_count)
    target = slot_expert % held * (groups * capacity) + slot_expert // held * capacity + position
    slot_gates = gates.reshape(-1)
    repeated = jnp.repeat(grad_out, chosen_count, axis=0)
    layout = (held, groups * capacity, width)
    returned = lax.all_to_all(
        saved_outputs.reshape(layout), "expert", split_axis=1, concat_axis=1, tiled=True
    )
    picked = returned.reshape(-1, width)[target]
    products = jnp.einsum("sd,sd->s", repeated, picked, preferred_element_type=jnp.float32)
    weighted = (slot_gates.astype(jnp.float32)[:, None] * repeated.astype(jnp.float32)).astype(
        jnp.bfloat16
    )
    buffer = jnp.zeros(saved_outputs.shape, jnp.bfloat16).at[target].set(weighted)
    expert_grad = lax.all_to_all(
        buffer.reshape(layout), "expert", split_axis=1, concat_axis=1, tiled=True
    ).reshape(-1, width)
    gate_grad = products.reshape(-1, chosen_count)
    gate_values = gates.astype(jnp.float32)
    blended = jnp.sum(gate_values * gate_grad, axis=1, keepdims=True)
    slot_grad = gate_values * (gate_grad - blended)
    onehot = (
        experts[:, :, None] == jnp.arange(expert_count, dtype=jnp.int32)[None, None, :]
    ).astype(jnp.float32)
    logit_grad = jnp.sum(onehot * slot_grad[:, :, None], axis=1).astype(jnp.bfloat16)
    partial_value = lax.dot_general(
        logit_grad, tokens, (((0,), (0,)), ((), ())), preferred_element_type=jnp.float32
    )
    summed = lax.psum(partial_value, ("dp", "expert"))
    scale_factor = float(lax.axis_size("dp") * groups * tokens.shape[0]) ** (-0.5)
    router_grad = summed * scale_factor
    input_grad = jnp.dot(logit_grad, router_weight, preferred_element_type=jnp.float32).astype(
        jnp.bfloat16
    )
    return (input_grad, router_grad, expert_grad)


def solution(mesh):
    return jax.shard_map(
        local,
        mesh=mesh,
        in_specs=(
            P(("dp", "expert"), None),
            P(("dp", "expert"), None),
            P(("dp", "expert"), None),
            P(("dp", "expert"), None),
            P(),
            P(("dp", "expert"), None),
        ),
        out_specs=(P(("dp", "expert"), None), P(), P(("dp", "expert"), None)),
        check_vma=False,
    )
```

profile of v0, /device:TPU:0, one launch (start us, length us, event | category | flops | bytes accessed | tf_op | source)
XLA Modules:
  0.0 228.8 jit_solution(14404547339752662202)
XLA Ops:
  7.2 8.7 %copy.40 = bf16[2,256,4096]{2,0,1:T(2,128)(2,1)} copy(bf16[2,256,4096]{2,1,0:T(8,128)(2,1)} %bitcast.20) | data formatting | bytes 8388608 | tf_op jit(solution)/shard_map/reshape | solution.py:27
  15.9 5.0 %all-to-all-start = ((bf16[2,256,4096]{2,0,1:T(2,128)(2,1)}), bf16[2,256,4096]{2,0,1:T(2,128)(2,1)}, u32[]{:S(2)}, u32[]{:S(2)}) async-start(bf16[2,256,4096]{2,0,1:T(2,128)(2,1)} %copy.40), calls=%async_computation | async-start | bytes 8388608 | tf_op jit(solution)/shard_map/all_to_all | solution.py:26
  21.0 0.1 eq.47
  21.2 0.1 eq.43
  21.3 0.1 reshape.177
  21.4 0.6 reduce-window.6
  22.0 0.2 slice_reduce_fusion
  22.3 3.5 %broadcast_in_dim.4 = bf16[128,2,4096]{2,1,0:T(2,128)(2,1)} broadcast(bf16[128,4096]{1,0:T(8,128)(2,1)S(1)} %copy-done.1), dimensions={0,2} | broadcast | bytes 3145728 | tf_op jit(solution)/shard_map/broadcast_in_dim | solution.py:24
  25.8 2.7 %reshape.179 = bf16[256,4096]{1,0:T(8,128)(2,1)S(1)} reshape(bf16[128,2,4096]{2,1,0:T(2,128)(2,1)} %broadcast_in_dim.4) | data formatting | bytes 4194304 | tf_op jit(solution)/shard_map/reshape | solution.py:24
  28.6 0.1 reshape.183
  28.9 6.1 %scatter_custom_fusion = bf16[512,4096]{1,0:T(8,128)(2,1)} fusion(s32[256]{0:T(256)S(1)} %bitcast.22, bf16[256,4096]{1,0:T(8,128)(2,1)S(1)} %reshape.179, f32[256]{0:T(256)S(1)} %reshape.183, bf16[]{:T(256)} %constant.44.clone.1), kind=kCustom, calls=%fused_computation.7 | custom fusion | flops 3145728 | bytes 6292482 | tf_op jit(solution)/shard_map/scatter | solution.py:34
  35.0 8.6 %copy.48 = bf16[2,256,4096]{2,0,1:T(2,128)(2,1)} copy(bf16[2,256,4096]{2,1,0:T(8,128)(2,1)} %bitcast.19) | data formatting | bytes 8388608 | tf_op jit(solution)/shard_map/reshape | solution.py:36
  43.6 26.2 %all-to-all-done = bf16[2,256,4096]{2,0,1:T(2,128)(2,1)} async-done(((bf16[2,256,4096]{2,0,1:T(2,128)(2,1)}), bf16[2,256,4096]{2,0,1:T(2,128)(2,1)}, u32[]{:S(2)}, u32[]{:S(2)}) %all-to-all-start) | async-done | bytes 4194336 | tf_op jit(solution)/shard_map/all_to_all | solution.py:26
  69.8 4.9 %all-to-all-start.1 = ((bf16[2,256,4096]{2,0,1:T(2,128)(2,1)}), bf16[2,256,4096]{2,0,1:T(2,128)(2,1)}, u32[]{:S(2)}, u32[]{:S(2)}) async-start(bf16[2,256,4096]{2,0,1:T(2,128)(2,1)} %copy.48), calls=%async_computation.1 | async-start | bytes 8388608 | tf_op jit(solution)/shard_map/all_to_all | solution.py:35
  74.8 7.1 %copy.41 = bf16[2,256,4096]{2,1,0:T(8,128)(2,1)} copy(bf16[2,256,4096]{2,0,1:T(2,128)(2,1)} %all-to-all-done) | data formatting | bytes 8388608 | tf_op jit(solution)/shard_map/all_to_all | solution.py:26
  81.9 8.0 %gather_fusion = bf16[256,4096]{1,0:T(8,128)(2,1)} fusion(bf16[512,4096]{1,0:T(8,128)(2,1)} %bitcast.18, s32[1024]{0:T(1024)S(1)} %pad_clamp_fusion), kind=kCustom, calls=%fused_computation | custom fusion | bytes 4195328 | tf_op jit(solution)/shard_map/gather | solution.py:29
  89.8 2.2 fusion
  92.1 0.1 reshape.180
  92.4 0.9 fusion.15
  93.3 1.4 convolution_convert_fusion
  94.8 28.4 %all-to-all-done.1 = bf16[2,256,4096]{2,0,1:T(2,128)(2,1)} async-done(((bf16[2,256,4096]{2,0,1:T(2,128)(2,1)}), bf16[2,256,4096]{2,0,1:T(2,128)(2,1)}, u32[]{:S(2)}, u32[]{:S(2)}) %all-to-all-start.1) | async-done | bytes 4194336 | tf_op jit(solution)/shard_map/all_to_all | solution.py:35
  123.2 7.1 %copy.49 = bf16[2,256,4096]{2,1,0:T(8,128)(2,1)} copy(bf16[2,256,4096]{2,0,1:T(2,128)(2,1)} %all-to-all-done.1) | data formatting | bytes 8388608 | tf_op jit(solution)/shard_map/all_to_all | solution.py:35
  130.3 90.1 %all-reduce.2.cloned.1.call-done = f32[8,4096]{1,0:T(8,128)} async-done(((f32[8,4096]{1,0:T(8,128)}), f32[8,4096]{1,0:T(8,128)}) %all-reduce.2.cloned.1.call-update) | async-done | bytes 131088 | tf_op jit(solution)/shard_map/psum | solution.py:49
  220.4 1.6 broadcast_multiply_fusion
  (24 shorter events, 0.6 us)
Async XLA Ops:
  7.2 85.2 %copy-start = (bf16[128,4096]{1,0:T(8,128)(2,1)S(1)}, bf16[128,4096]{1,0:T(8,128)(2,1)}, u32[]{:S(2)}) copy-start(bf16[128,4096]{1,0:T(8,128)(2,1)} %param.6) | copy-start | bytes 3145732
  15.9 5.0 %copy-start.4 = (s32[128,2]{0,1:T(2,128)S(1)}, s32[128,2]{0,1:T(2,128)}, u32[]{:S(2)}) copy-start(s32[128,2]{0,1:T(2,128)} %param.8) | copy-start | bytes 3076
  15.9 6.4 %copy-start.1 = (bf16[128,4096]{1,0:T(8,128)(2,1)S(1)}, bf16[128,4096]{1,0:T(8,128)(2,1)}, u32[]{:S(2)}) copy-start(bf16[128,4096]{1,0:T(8,128)(2,1)} %param.7) | copy-start | bytes 3145732
  15.9 53.9 %all-to-all-start = ((bf16[2,256,4096]{2,0,1:T(2,128)(2,1)}), bf16[2,256,4096]{2,0,1:T(2,128)(2,1)}, u32[]{:S(2)}, u32[]{:S(2)}) async-start(bf16[2,256,4096]{2,0,1:T(2,128)(2,1)} %copy.40), calls=%async_computation | async-start | bytes 8388608 | tf_op jit(solution)/shard_map/all_to_all | solution.py:26
  20.9 7.6 %copy-start.3 = (bf16[128,2]{0,1:T(2,128)(2,1)S(1)}, bf16[128,2]{0,1:T(2,128)(2,1)}, u32[]{:S(2)}) copy-start(bf16[128,2]{0,1:T(2,128)(2,1)} %param.9) | copy-start | bytes 1540
  69.8 53.4 %all-to-all-start.1 = ((bf16[2,256,4096]{2,0,1:T(2,128)(2,1)}), bf16[2,256,4096]{2,0,1:T(2,128)(2,1)}, u32[]{:S(2)}, u32[]{:S(2)}) async-start(bf16[2,256,4096]{2,0,1:T(2,128)(2,1)} %copy.48), calls=%async_computation.1 | async-start | bytes 8388608 | tf_op jit(solution)/shard_map/all_to_all | solution.py:35
  74.7 145.7 %all-reduce.2.cloned.1.call-start = ((), (), s32[]{:S(2)}) async-start(), calls=%async_computation.2 | async-start | bytes 262144 | tf_op jit(solution)/shard_map/psum | solution.py:49
  89.8 3.5 %copy-start.2 = (bf16[8,4096]{1,0:T(8,128)(2,1)S(1)}, bf16[8,4096]{1,0:T(8,128)(2,1)}, u32[]{:S(2)}) copy-start(bf16[8,4096]{1,0:T(8,128)(2,1)} %param.10) | copy-start | bytes 196612
Sparse Core Ops, SparseCore 0:
  93.4 126.8 all-reduce.1
where the time goes:
time: 229 us
  waiting for transfers between devices  145 us (63%)
  local copies, waits for them, and re-layouts  46.9 us (20%)
  between operations  14.2 us (6%)
  other arithmetic  10.7 us (5%)
  starting transfers between devices  9.97 us (4%)
  matrix products  2.36 us (1%)
    psum x1, waiting for transfers between devices, local(): summed = lax.psum(partial_value, ('dp', 'expert'))  90.1 us
    all_to_all x1, waiting for transfers between devices, local(): lax.all_to_all(buffer.reshape(layout), 'expert', split_axis=1, concat_axi...  28.4 us
    all_to_all x1, waiting for transfers between devices, local(): lax.all_to_all(saved_outputs.reshape(layout), 'expert', split_axis=1, con...  26.2 us
    reshape x1, local copies, waits for them, and re-layouts, local(): saved_outputs.reshape(layout)  8.69 us
    reshape x1, local copies, waits for them, and re-layouts, local(): buffer.reshape(layout)  8.56 us
    gather x1, local copies, waits for them, and re-layouts, local(): picked = returned.reshape(-1, width)[target]  7.96 us
    all_to_all x1, local copies, waits for them, and re-layouts, local(): lax.all_to_all(buffer.reshape(layout), 'expert', split_axis=1, concat_axi...  7.13 us
    all_to_all x1, local copies, waits for them, and re-layouts, local(): lax.all_to_all(saved_outputs.reshape(layout), 'expert', split_axis=1, con...  7.11 us
  transfers between devices with their start and end apart: 3, of which 3 were waited for; matrix products, arithmetic and copies ran while one was open for 22% of the time, Pallas kernels for 0%

commit v1 on v0

--- a/solution.py
+++ b/solution.py
@@ -46,7 +46,7 @@
     partial_value = lax.dot_general(
         logit_grad, tokens, (((0,), (0,)), ((), ())), preferred_element_type=jnp.float32
     )
-    summed = lax.psum(partial_value, ("dp", "expert"))
+    summed = jnp.sum(lax.all_gather(partial_value, ("dp", "expert")), axis=0)
     scale_factor = float(lax.axis_size("dp") * groups * tokens.shape[0]) ** (-0.5)
     router_grad = summed * scale_factor
     input_grad = jnp.dot(logit_grad, router_weight, preferred_element_type=jnp.float32).astype(

time: 229 us -> 178 us (0.78)
  waiting for transfers between devices: 145 us -> 40.9 us
  blocking collectives: 0 us -> 60 us
  starting transfers between devices: 9.97 us -> 5.21 us
  local copies, waits for them, and re-layouts: 46.9 us -> 42.7 us
    psum x1 -> x0, waiting for transfers between devices: 90.1 us -> none  [local(): summed = lax.psum(partial_value, ('dp', 'expert'))]
    all_to_all x0 -> x1, blocking collectives: none -> 60 us  [local(): lax.all_to_all(buffer.reshape(layout), 'expert', split_axis=1, concat_axi...]
    all_to_all x1 -> x0, waiting for transfers between devices: 28.4 us -> none  [local(): lax.all_to_all(buffer.reshape(layout), 'expert', split_axis=1, concat_axi...]
    all_to_all x1, waiting for transfers between devices: 26.2 us -> 40.9 us  [local(): lax.all_to_all(saved_outputs.reshape(layout), 'expert', split_axis=1, con...]
    all_to_all x1 -> x0, starting transfers between devices: 4.94 us -> none  [local(): lax.all_to_all(buffer.reshape(layout), 'expert', split_axis=1, concat_axi...]
    reduce_sum x0 -> x1, other arithmetic: none -> 2.4 us  [local(): summed = jnp.sum(lax.all_gather(partial_value, ('dp', 'expert')), axis=0)]
  transfers between devices with their start and end apart: 3 -> 2, of which waited for: 3 -> 1; matrix products, arithmetic and copies ran while one was open for 22% -> 15% of each run, Pallas kernels for 0% -> 0%
where the time goes in v1:
time: 178 us
  blocking collectives  60 us (34%)
  local copies, waits for them, and re-layouts  42.7 us (24%)
  waiting for transfers between devices  40.9 us (23%)
  between operations  14.1 us (8%)
  other arithmetic  12.5 us (7%)
  starting transfers between devices  5.21 us (3%)
  matrix products  2.36 us (1%)
    all_to_all x1, blocking collectives, local(): lax.all_to_all(buffer.reshape(layout), 'expert', split_axis=1, concat_axi...  60 us
    all_to_all x1, waiting for transfers between devices, local(): lax.all_to_all(saved_outputs.reshape(layout), 'expert', split_axis=1, con...  40.9 us
    reshape x1, local copies, waits for them, and re-layouts, local(): saved_outputs.reshape(layout)  8.69 us
    gather x1, local copies, waits for them, and re-layouts, local(): picked = returned.reshape(-1, width)[target]  7.96 us
    all_to_all x1, local copies, waits for them, and re-layouts, local(): lax.all_to_all(saved_outputs.reshape(layout), 'expert', split_axis=1, con...  7.11 us
    reshape x1, local copies, waits for them, and re-layouts, local(): buffer.reshape(layout)  6.59 us
    scatter x1, other arithmetic, local(): jnp.zeros(saved_outputs.shape, jnp.bfloat16).at[target].set(weighted)  6.36 us
    all_to_all x1, starting transfers between devices, local(): lax.all_to_all(saved_outputs.reshape(layout), 'expert', split_axis=1, con...  4.99 us
  transfers between devices with their start and end apart: 2, of which 1 were waited for; matrix products, arithmetic and copies ran while one was open for 15% of the time, Pallas kernels for 0%

profile of v1, /device:TPU:0, one launch (start us, length us, event | category | flops | bytes accessed | tf_op | source)
XLA Modules:
  0.0 177.7 jit_solution(8461542470771208002)
XLA Ops:
  7.2 8.7 %copy.40 = bf16[2,256,4096]{2,0,1:T(2,128)(2,1)} copy(bf16[2,256,4096]{2,1,0:T(8,128)(2,1)} %bitcast.22) | data formatting | bytes 8388608 | tf_op jit(solution)/shard_map/reshape | solution.py:27
  15.9 5.0 %all-to-all-start = ((bf16[2,256,4096]{2,0,1:T(2,128)(2,1)}), bf16[2,256,4096]{2,0,1:T(2,128)(2,1)}, u32[]{:S(2)}, u32[]{:S(2)}) async-start(bf16[2,256,4096]{2,0,1:T(2,128)(2,1)} %copy.40), calls=%async_computation | async-start | bytes 8388608 | tf_op jit(solution)/shard_map/all_to_all | solution.py:26
  20.9 0.2 all-gather.3.cloned.1.call-start
  21.2 0.1 eq.47
  21.4 0.1 eq.43
  21.5 0.1 reshape.177
  21.7 0.6 reduce-window.6
  22.3 0.2 slice_reduce_fusion
  22.5 3.5 %broadcast_in_dim.4 = bf16[128,2,4096]{2,1,0:T(2,128)(2,1)} broadcast(bf16[128,4096]{1,0:T(8,128)(2,1)S(1)} %copy-done.1), dimensions={0,2} | broadcast | bytes 3145728 | tf_op jit(solution)/shard_map/broadcast_in_dim | solution.py:24
  26.0 2.7 %reshape.179 = bf16[256,4096]{1,0:T(8,128)(2,1)S(1)} reshape(bf16[128,2,4096]{2,1,0:T(2,128)(2,1)} %broadcast_in_dim.4) | data formatting | bytes 4194304 | tf_op jit(solution)/shard_map/reshape | solution.py:24
  28.8 40.9 %all-to-all-done = bf16[2,256,4096]{2,0,1:T(2,128)(2,1)} async-done(((bf16[2,256,4096]{2,0,1:T(2,128)(2,1)}), bf16[2,256,4096]{2,0,1:T(2,128)(2,1)}, u32[]{:S(2)}, u32[]{:S(2)}) %all-to-all-start) | async-done | bytes 4194336 | tf_op jit(solution)/shard_map/all_to_all | solution.py:26
  69.8 7.1 %copy.41 = bf16[2,256,4096]{2,1,0:T(8,128)(2,1)} copy(bf16[2,256,4096]{2,0,1:T(2,128)(2,1)} %all-to-all-done) | data formatting | bytes 8388608 | tf_op jit(solution)/shard_map/all_to_all | solution.py:26
  76.9 8.0 %gather_fusion = bf16[256,4096]{1,0:T(8,128)(2,1)} fusion(bf16[512,4096]{1,0:T(8,128)(2,1)} %bitcast.20, s32[1024]{0:T(1024)S(1)} %pad_clamp_fusion), kind=kCustom, calls=%fused_computation | custom fusion | bytes 4195328 | tf_op jit(solution)/shard_map/gather | solution.py:29
  84.8 2.2 %fusion = f32[256]{0:T(256)S(1)} fusion(bf16[256,4096]{1,0:T(8,128)(2,1)S(1)} %reshape.179, bf16[256,4096]{1,0:T(8,128)(2,1)} %gather_fusion), kind=kLoop, calls=%fused_computation.5 | loop fusion | flops 4194048 | bytes 4195328 | tf_op jit(solution)/shard_map/sd,sd->s/dot_general | solution.py:30
  87.1 0.1 reshape.180
  87.3 0.9 fusion.15
  88.4 0.1 reshape.183
  88.5 6.4 %scatter_custom_fusion = bf16[512,4096]{1,0:T(8,128)(2,1)} fusion(s32[256]{0:T(256)S(1)} %bitcast.25, bf16[256,4096]{1,0:T(8,128)(2,1)S(1)} %reshape.179, f32[256]{0:T(256)S(1)} %reshape.183, bf16[]{:T(256)} %constant.44.clone.1), kind=kCustom, calls=%fused_computation.8 | custom fusion | flops 3145728 | bytes 6292482 | tf_op jit(solution)/shard_map/scatter | solution.py:34
  94.9 6.6 %copy.48 = bf16[2,256,4096]{2,0,1:T(2,128)(2,1)S(1)} copy(bf16[2,256,4096]{2,1,0:T(8,128)(2,1)} %bitcast.21) | data formatting | bytes 8388608 | tf_op jit(solution)/shard_map/reshape | solution.py:36
  101.5 60.0 %all_to_all.10 = bf16[2,256,4096]{2,0,1:T(2,128)(2,1)S(1)} all-to-all(bf16[2,256,4096]{2,0,1:T(2,128)(2,1)S(1)} %copy.48), channel_id=1, replica_groups=mesh['dp'=8,'expert'=4] {'expert'}, dimensions={1} | all-to-all | bytes 8388608 | tf_op jit(solution)/shard_map/all_to_all | solution.py:35
  161.5 4.9 %copy.49 = bf16[2,256,4096]{2,1,0:T(8,128)(2,1)} copy(bf16[2,256,4096]{2,0,1:T(2,128)(2,1)S(1)} %all_to_all.10) | data formatting | bytes 8388608 | tf_op jit(solution)/shard_map/all_to_all | solution.py:35
  166.4 1.4 convolution_convert_fusion
  167.8 2.4 %bitcast_reduce_fusion = f32[8,4096]{1,0:T(8,128)S(1)} fusion(f32[256,4096]{1,0:T(8,128)} %all-gather.3.cloned.1.call-done), kind=kLoop, calls=%fused_computation.7 | loop fusion | flops 1015808 | bytes 4325376 | tf_op jit(solution)/shard_map/reduce_sum | solution.py:49
  170.2 0.7 broadcast_multiply_fusion
  (24 shorter events, 0.5 us)
Async XLA Ops:
  7.2 80.2 %copy-start = (bf16[128,4096]{1,0:T(8,128)(2,1)S(1)}, bf16[128,4096]{1,0:T(8,128)(2,1)}, u32[]{:S(2)}) copy-start(bf16[128,4096]{1,0:T(8,128)(2,1)} %param.6) | copy-start | bytes 3145732
  15.9 5.2 %copy-start.4 = (s32[128,2]{0,1:T(2,128)S(1)}, s32[128,2]{0,1:T(2,128)}, u32[]{:S(2)}) copy-start(s32[128,2]{0,1:T(2,128)} %param.8) | copy-start | bytes 3076
  15.9 6.6 %copy-start.1 = (bf16[128,4096]{1,0:T(8,128)(2,1)S(1)}, bf16[128,4096]{1,0:T(8,128)(2,1)}, u32[]{:S(2)}) copy-start(bf16[128,4096]{1,0:T(8,128)(2,1)} %param.7) | copy-start | bytes 3145732
  15.9 53.9 %all-to-all-start = ((bf16[2,256,4096]{2,0,1:T(2,128)(2,1)}), bf16[2,256,4096]{2,0,1:T(2,128)(2,1)}, u32[]{:S(2)}, u32[]{:S(2)}) async-start(bf16[2,256,4096]{2,0,1:T(2,128)(2,1)} %copy.40), calls=%async_computation | async-start | bytes 8388608 | tf_op jit(solution)/shard_map/all_to_all | solution.py:26
  20.9 146.9 %all-gather.3.cloned.1.call-start = ((), (), s32[]{:S(2)}) async-start(), calls=%async_computation.2 | async-start | bytes 4325376 | tf_op jit(solution)/shard_map/all_gather | solution.py:49
  84.8 2.4 %copy-start.3 = (bf16[128,2]{0,1:T(2,128)(2,1)S(1)}, bf16[128,2]{0,1:T(2,128)(2,1)}, u32[]{:S(2)}) copy-start(bf16[128,2]{0,1:T(2,128)(2,1)} %param.9) | copy-start | bytes 1540
  161.5 4.9 %copy-start.2 = (bf16[8,4096]{1,0:T(8,128)(2,1)S(1)}, bf16[8,4096]{1,0:T(8,128)(2,1)}, u32[]{:S(2)}) copy-start(bf16[8,4096]{1,0:T(8,128)(2,1)} %param.10) | copy-start | bytes 196612
Sparse Core Ops, SparseCore 0:
  88.4 70.3 all-gather.2
